TPU v7x, 32 devices: a whole 2x2x4 slice. The times are simulated.
32 devices in a mesh: groups: 2 (over y), fsdp: 4 (over z), expert: 4 (over x, core).
Axes of the slice: x: 2, y: 2, z: 4, core: 2. Of those that a mesh axis runs over, the one named last changes fastest.
Arguments:
- queries: bfloat16 [512, 2048], P(('groups', 'fsdp'), 'expert'), parts along dimension 0, may hold values from -14 to 14
- keys: bfloat16 [8, 2048, 512], P(('groups', 'fsdp'), None, 'expert'), parts along dimension 0, may hold values from -14 to 14
- values: bfloat16 [8, 2048, 512], P(('groups', 'fsdp'), None, 'expert'), parts along dimension 0, may hold values from -4 to 4
- out_weight: bfloat16 [2048, 4096], P('expert', 'fsdp'), may hold values from -0.5 to 0.5
- residual: bfloat16 [512, 4096], P(('groups', 'fsdp')), parts along dimension 0, may hold values from -3 to 3
- norm_gain: float32 [4096], replicated, may hold values from 0.5 to 1.5
- route_ids: int32 [512, 2], P(('groups', 'fsdp')), parts along dimension 0, may hold values from 0 to 7, as said below
- route_slots: int32 [512, 2], P(('groups', 'fsdp')), parts along dimension 0, may hold values from 0 to 23, as said below
- route_weights: int32 [512, 2], P(('groups', 'fsdp')), parts along dimension 0, may hold values from 1 to 65535, as said below
- w_gate: bfloat16 [8, 4096, 7168], P('expert', None, 'fsdp'), may hold values from -0.09375 to 0.09375
- w_up: bfloat16 [8, 4096, 7168], P('expert', None, 'fsdp'), may hold values from -0.09375 to 0.09375
- w_down: bfloat16 [8, 7168, 4096], P('expert', 'fsdp'), may hold values from -0.0625 to 0.0625
Outputs:
- layer_out: bfloat16 [512, 4096], P(('groups', 'fsdp'), 'expert'), parts along dimension 0
There are 2 independent parts, one for each index of `groups`. A program takes and returns all parts, laid end to end along the dimension named above; an argument that names none is the same for every part. Nothing has to cross between parts.
Inputs may be any that keep to these rules, and one draw needn't show every extreme that they name: `route_ids`: each row names two different experts. Among the rows of one block, no expert is named more than 24 times and no group of experts 2 g and 2 g + 1 more than 36 times; one expert, the same for all blocks, is named exactly 24 times in every block and its group exactly 36 times; every expert is named in every block. `route_slots`: within one block, the routes to one expert hold the slots 0 to their count - 1, each once. `route_weights`: the two entries of a row sum to 65536.
All inputs are finite; a program needn't handle non-finite values.
Results may differ from a plain program's by a relative error of at most 0.02.
Values may be sent and summed in bfloat16 or wider, within the bound.
No kernel may reach another device: no remote copies, remote signals or barrier semaphores. Data moves between devices by JAX's collectives and lax.ppermute only.
A program may use at most 192 MiB of HBM per device.

v0:
```python
import jax
import jax.numpy as jnp
from jax import lax
from jax.sharding import PartitionSpec as P

HEAD_DIM = 128
GCAP = 36
eps = 1e-05


def attend(queries, keys, values):
    block = queries.shape[0]
    context = keys.shape[1]
    kv_dev = keys.shape[2] // HEAD_DIM
    heads_dev = queries.shape[1] // HEAD_DIM
    group = heads_dev // kv_dev
    query_heads = queries.reshape(block, kv_dev, group, HEAD_DIM)
    key_heads = keys[0].reshape(context, kv_dev, HEAD_DIM)
    value_heads = values[0].reshape(context, kv_dev, HEAD_DIM)
    scores = jnp.einsum(
        "qcgd,kcd->cgqk", query_heads, key_heads, preferred_element_type=jnp.float32
    ) * HEAD_DIM ** (-0.5)
    key_pos = jnp.arange(context)
    query_pos = context - block + jnp.arange(block)
    allowed = key_pos[None, :] <= query_pos[:, None]
    masked = jnp.where(allowed, scores, -1e30)
    highest = jnp.max(masked, axis=-1, keepdims=True)
    weights = jnp.where(allowed, jnp.exp(masked - highest), 0.0)
    probs = (weights / jnp.sum(weights, axis=-1, keepdims=True)).astype(jnp.bfloat16)
    heads_out = jnp.einsum("cgqk,kcd->qcgd", probs, value_heads, preferred_element_type=jnp.float32)
    return heads_out.astype(jnp.bfloat16).reshape(block, heads_dev * HEAD_DIM)


def per_device(
    queries,
    keys,
    values,
    out_weight,
    residual,
    norm_gain,
    route_ids,
    route_slots,
    route_weights,
    w_gate,
    w_up,
    w_down,
):
    heads_out = attend(queries, keys, values)
    partial_attn = jnp.dot(
        heads_out,
        lax.all_gather(out_weight, "fsdp", axis=1, tiled=True),
        preferred_element_type=jnp.float32,
    )
    attn = lax.psum(partial_attn.astype(jnp.bfloat16), "expert").astype(jnp.float32)
    hstate = (residual.astype(jnp.float32) + attn).astype(jnp.bfloat16)
    state = hstate.astype(jnp.float32)
    scale = lax.rsqrt(jnp.mean(state * state, axis=-1, keepdims=True) + eps)
    normed = (state * scale * norm_gain).astype(jnp.bfloat16)
    group_index = lax.axis_index("expert")
    first_expert = 2 * group_index
    within = route_ids - first_expert
    in_group = (within >= 0) & (within < 2)
    lead_count = jnp.sum((route_ids == first_expert).astype(jnp.int32))
    target = jnp.where(in_group, route_slots + within * lead_count, -1)
    row_ids = jnp.arange(GCAP)
    one_hot = (
        (target[None, :, 0] == row_ids[:, None]) | (target[None, :, 1] == row_ids[:, None])
    ).astype(jnp.bfloat16)
    dispatch = jnp.dot(one_hot, normed, preferred_element_type=jnp.float32).astype(jnp.bfloat16)
    second = (row_ids >= lead_count).astype(jnp.bfloat16)
    rows = lax.all_gather(dispatch, "fsdp", axis=0, tiled=True)
    labels = lax.all_gather(second, "fsdp", axis=0, tiled=True)
    gate = jnp.einsum("nd,edf->enf", rows, w_gate, preferred_element_type=jnp.float32)
    upper = jnp.einsum("nd,edf->enf", rows, w_up, preferred_element_type=jnp.float32)
    labels_f = labels.astype(jnp.float32)
    keep = jnp.stack([1.0 - labels_f, labels_f], axis=0)[:, :, None]
    values_new = (jax.nn.silu(gate) * upper * keep).astype(jnp.bfloat16)
    flat_out = lax.psum_scatter(
        jnp.einsum("enf,efd->nd", values_new, w_down, preferred_element_type=jnp.float32).astype(
            jnp.bfloat16
        ),
        "fsdp",
        scatter_dimension=0,
        tiled=True,
    ).astype(jnp.float32)
    row_index = route_slots + within * lead_count
    safe_index = jnp.where(in_group, row_index, 0)
    shares = jnp.where(in_group, route_weights.astype(jnp.float32) / 65536.0, 0.0)
    picked = jnp.take(flat_out, safe_index, axis=0)
    contrib = jnp.sum(shares[:, :, None] * picked, axis=1)
    moe = lax.psum_scatter(
        contrib.astype(jnp.bfloat16), "expert", scatter_dimension=1, tiled=True
    ).astype(jnp.float32)
    width = moe.shape[1]
    own_state = lax.dynamic_slice_in_dim(hstate, group_index * width, width, 1)
    return (own_state.astype(jnp.float32) + moe).astype(jnp.bfloat16)


def solution(mesh):
    in_specs = (
        P(("groups", "fsdp"), "expert"),
        P(("groups", "fsdp"), None, "expert"),
        P(("groups", "fsdp"), None, "expert"),
        P("expert", "fsdp"),
        P(("groups", "fsdp"), None),
        P(),
        P(("groups", "fsdp"), None),
        P(("groups", "fsdp"), None),
        P(("groups", "fsdp"), None),
        P("expert", None, "fsdp"),
        P("expert", None, "fsdp"),
        P("expert", "fsdp", None),
    )
    out_specs = P(("groups", "fsdp"), "expert")
    return jax.shard_map(
        per_device, mesh=mesh, in_specs=in_specs, out_specs=out_specs, check_vma=False
    )
```

profile of v0, /device:TPU:0, one launch (start us, length us, event | category | flops | bytes accessed | tf_op | source)
XLA Modules:
  0.0 273.5 jit_solution(8926764271031604778)
XLA Ops:
  6.5 0.0 copy-start
  6.5 0.0 all-gather.4.cloned.1.call-start
  6.5 0.7 all-gather.4.cloned.1.call-update
  7.3 0.0 all-reduce.5.cloned.1.call-start
  7.3 0.1 iota_compare_fusion
  7.5 0.1 copy-done
  7.6 0.0 copy-start.8
  7.6 1.5 fusion.39
  9.1 0.5 fusion.13
  9.6 0.0 copy-done.8
  9.6 0.0 copy-start.4
  9.6 0.0 copy-start.7
  9.6 0.7 fusion.14
  10.3 0.1 copy.23
  10.4 0.0 copy-done.4
  10.4 0.6 fusion.35
  11.1 0.0 copy-done.7
  11.1 81.3 %all-gather.4.cloned.1.call-done = bf16[512,4096]{1,0:T(8,128)(2,1)} async-done(((bf16[512,1024]{1,0:T(8,128)(2,1)}), bf16[512,4096]{1,0:T(8,128)(2,1)}) %all-gather.4.cloned.1.call-update) | async-done | bytes 4194320 | tf_op jit(solution)/shard_map/all_gather | solution.py:51
  92.4 0.0 copy-start.5
  92.4 0.0 copy-start.3
  92.4 3.9 %convolution_convert_fusion = bf16[64,4096]{1,0:T(8,128)(2,1)} fusion(bf16[512,4096]{1,0:T(8,128)(2,1)} %all-gather.4.cloned.1.call-done, bf16[8,8,4,128]{3,2,1,0:T(4,128)(2,1)S(1)} %bitcast.74), kind=kOutput, calls=%fused_computation.3 | convolution fusion | flops 268697600 | bytes 4784128 | tf_op jit(solution)/shard_map/dot_general | solution.py:49
  96.3 0.0 copy-start.9
  96.3 0.0 copy-start.6
  96.3 0.0 all-reduce.5.cloned.1.call-update
  96.3 0.0 all-gather.6.cloned.1.call-start
  96.4 0.0 copy-done.5
  96.4 0.7 broadcast_select_fusion
  97.0 31.3 %all-reduce.5.cloned.1.call-done = bf16[64,4096]{1,0:T(8,128)(2,1)} async-done(((bf16[64,4096]{1,0:T(8,128)(2,1)}), bf16[64,4096]{1,0:T(8,128)(2,1)}) %all-reduce.5.cloned.1.call-update) | async-done | bytes 524304 | tf_op jit(solution)/shard_map/psum | solution.py:54
  128.4 0.0 copy-done.3
  128.4 1.3 fusion.15
  129.7 0.0 copy-start.2
  129.7 0.0 copy-done.9
  129.7 1.1 fusion.2
  130.8 0.0 all-gather.6.cloned.1.call-update
  130.8 0.0 reduce-scatter.4.cloned.1.call-start
  130.9 0.0 copy-done.6
  130.9 0.7 fusion.38
  132.2 0.7 compare_convert_fusion
  132.8 0.2 dynamic-update-slice
  133.1 11.8 %all-reduce = bf16[144]{0:T(256)(128)(2,1)S(1)} all-reduce(bf16[144]{0:T(256)(128)(2,1)S(1)} %dynamic-update-slice), channel_id=1, replica_groups=mesh['groups'=2,'fsdp'=4,'expert'=4] {'fsdp'}, use_global_device_ids=true, to_apply=%add | all-reduce | flops 144 | bytes 576
  144.9 0.7 compare_and_fusion
  145.5 0.1 copy.26
  145.6 0.1 reshape.63
  145.8 0.1 copy.25
  145.9 0.1 copy.24
  146.7 17.0 %all-gather.6.cloned.1.call-done = bf16[4,36,4096]{2,1,0:T(8,128)(2,1)} async-done(((bf16[1,36,4096]{2,1,0:T(8,128)(2,1)}), bf16[4,36,4096]{2,1,0:T(8,128)(2,1)}) %all-gather.6.cloned.1.call-update) | async-done | bytes 1179664 | tf_op jit(solution)/shard_map/all_gather | solution.py:71
  163.6 2.2 reshape.80
  165.9 12.0 %convolution_bitcast_fusion.2 = f32[2,144,1792]{2,1,0:T(8,128)S(1)} fusion(bf16[144,4096,1]{1,0,2:T(8,128)(2,1)} %reshape.80, bf16[2,4096,1792]{2,1,0:T(8,128)(2,1)} %param.21), kind=kOutput, calls=%fused_computation.7 | convolution fusion | flops 4227858432 | bytes 32604160 | tf_op jit(solution)/shard_map/nd,edf->enf/dot_general | solution.py:73
  177.9 0.0 copy-done.2
  177.9 22.2 %fusion.1 = bf16[144,4096]{1,0:T(8,128)(2,1)} fusion(bf16[2,1792,4096]{2,1,0:T(8,128)(2,1)} %param.23, bf16[144,4096,1]{1,0,2:T(8,128)(2,1)} %reshape.80, bf16[2,4096,1792]{2,1,0:T(8,128)(2,1)} %param.22, f32[2,144,1792]{2,1,0:T(8,128)S(1)} %convolution_bitcast_fusion.2, f32[2,144]{1,0:T(2,128)S(1)} %pad_maximum_fusion), kind=kOutput, calls=%fused_computation.2 | convolution fusion | flops 8459919360 | bytes 63145088 | tf_op jit(solution)/shard_map/enf,efd->nd/dot_general | solution.py:79
  200.1 29.1 %fusion = bf16[40,4096]{1,0:T(8,128)(2,1)S(1)} fusion(bf16[144,4096]{1,0:T(8,128)(2,1)} %fusion.1), kind=kCustom, calls=%all-reduce-scatter | all-reduce-scatter fusion | flops 655361 | bytes 1507840
  229.2 1.8 collective-permute-start
  231.0 2.3 collective-permute-done
  233.3 0.4 concatenate
  233.7 0.1 dynamic-slice_convert_fusion
  233.8 1.3 gather_fusion
  235.1 0.0 copy-start.1
  235.2 2.3 reshape.62
  237.4 6.0 %multiply_reduce_fusion = bf16[64,4096]{1,0:T(8,128)(2,1)} fusion(f32[64,2,4096]{2,1,0:T(2,128)} %reshape.62, pred[64,2]{1,0:T(8,128)(4,1)S(1)} %copy.25, f32[64,2]{1,0:T(8,128)S(1)} %copy.24), kind=kLoop, calls=%fused_computation.14 | loop fusion | flops 1310720 | bytes 2622080 | tf_op jit(solution)/shard_map/reduce_sum | solution.py:90
  243.5 0.0 reduce-scatter.4.cloned.1.call-update
  243.5 21.9 %reduce-scatter.4.cloned.1.call-done = bf16[64,1024]{1,0:T(8,128)(2,1)} async-done(((bf16[64,4096]{1,0:T(8,128)(2,1)}), bf16[64,1024]{1,0:T(8,128)(2,1)}) %reduce-scatter.4.cloned.1.call-update) | async-done | bytes 131088 | tf_op jit(solution)/shard_map/reduce_scatter | solution.py:91
  265.4 1.7 add_convert_fusion.1
  267.0 0.0 copy-done.1
  (10 shorter events, 0.1 us)
Async XLA Ops:
  6.5 1.0 copy-start
  6.5 85.9 %all-gather.4.cloned.1.call-start = ((), (), s32[]{:S(2)}) async-start(), calls=%async_computation.1 | async-start | bytes 5242880 | tf_op jit(solution)/shard_map/all_gather | solution.py:51
  7.3 121.1 %all-reduce.5.cloned.1.call-start = ((), (), s32[]{:S(2)}) async-start(), calls=%async_computation.2 | async-start | bytes 1048576 | tf_op jit(solution)/shard_map/psum | solution.py:54
  7.6 2.0 copy-start.8
  9.6 0.8 copy-start.4
  9.6 1.5 copy-start.7
  92.4 4.0 %copy-start.5 = (s32[64,2]{0,1:T(2,128)S(1)}, s32[64,2]{0,1:T(2,128)}, u32[]{:S(2)}) copy-start(s32[64,2]{0,1:T(2,128)} %param.19) | copy-start | bytes 1540
  92.4 36.0 %copy-start.3 = (bf16[64,4096]{1,0:T(8,128)(2,1)S(1)}, bf16[64,4096]{1,0:T(8,128)(2,1)}, u32[]{:S(2)}) copy-start(bf16[64,4096]{1,0:T(8,128)(2,1)} %param.16) | copy-start | bytes 1572868
  96.3 33.4 %copy-start.9 = (f32[4096]{0:T(1024)S(1)}, f32[4096]{0:T(1024)}, u32[]{:S(2)}) copy-start(f32[4096]{0:T(1024)} %param.17) | copy-start | bytes 49156
  96.3 34.6 %copy-start.6 = (u32[32]{0:T(128)S(1)}, u32[32]{0:T(128)}, u32[]{:S(2)}) copy-start(u32[32]{0:T(128)} %constant.60) | copy-start | bytes 388
  96.3 67.3 %all-gather.6.cloned.1.call-start = ((), (), s32[]{:S(2)}) async-start(), calls=%async_computation.4 | async-start | bytes 1638400 | tf_op jit(solution)/shard_map/all_gather | solution.py:71
  129.7 48.2 %copy-start.2 = (bf16[64,4096]{1,0:T(8,128)(2,1)}, bf16[64,4096]{1,0:T(8,128)(2,1)S(1)}, u32[]{:S(2)}) copy-start(bf16[64,4096]{1,0:T(8,128)(2,1)S(1)} %get-tuple-element.10) | copy-start | bytes 1572868
  130.8 134.5 %reduce-scatter.4.cloned.1.call-start = ((), (), s32[]{:S(2)}) async-start(), calls=%async_computation.3 | async-start | bytes 655360 | tf_op jit(solution)/shard_map/reduce_scatter | solution.py:91
  229.2 4.1 %collective-permute-start = (bf16[12,4096]{1,0:T(8,128)(2,1)S(1)}, bf16[12,4096]{1,0:T(8,128)(2,1)S(1)}, u32[]{:S(2)}, u32[]{:S(2)}) collective-permute-start(bf16[12,4096]{1,0:T(8,128)(2,1)S(1)} %slice.10), channel_id=1, source_target_pairs={{0,4},{4,8},{8,12},{1,5},{5,9},{9,13},{2,6},{6,10},{10,14},{3,7},{... | collective-permute-start | bytes 294920
  235.1 31.9 %copy-start.1 = (bf16[1,2048,128]{2,1,0:T(8,128)(2,1)S(1)}, bf16[1,2048,128]{2,1,0:T(8,128)(2,1)}, u32[]{:S(2)}) copy-start(bf16[1,2048,128]{2,1,0:T(8,128)(2,1)} %param.13) | copy-start | bytes 1572868
Sparse Core Ops, SparseCore 0:
  8.9 83.4 all-gather.3
  96.4 31.8 all-reduce.4
  130.9 32.6 all-gather.5
  243.6 21.6 reduce-scatter.3
where the time goes:
time: 274 us
  waiting for transfers between devices  155 us (57%)
  matrix products  41.3 us (15%)
  blocking collectives  40.8 us (15%)
  between operations  14.7 us (5%)
  other arithmetic  12.4 us (5%)
  local copies, waits for them, and re-layouts  7.87 us (3%)
    all_gather x1, waiting for transfers between devices, per_device(): lax.all_gather(out_weight, 'fsdp', axis=1, tiled=True)  81.3 us
    unnamed x2, blocking collectives  40.8 us
    psum x1, waiting for transfers between devices, per_device(): lax.psum(partial_attn.astype(jnp.bfloat16), 'expert').astype(jnp.float32)  31.3 us
    dot_general x1, matrix products, per_device(): jnp.einsum('enf,efd->nd', values_new, w_down, preferred_element_type=jnp....  22.2 us
    reduce_scatter x1, waiting for transfers between devices, per_device(): lax.psum_scatter(contrib.astype(jnp.bfloat16), 'expert', scatter_dimensio...  21.9 us
    all_gather x1, waiting for transfers between devices, per_device(): rows = lax.all_gather(dispatch, 'fsdp', axis=0, tiled=True)  17 us
    dot_general x1, matrix products, per_device(): jnp.einsum('nd,edf->enf', rows, w_gate, preferred_element_type=jnp.float32)  12 us
    reduce_sum x1, other arithmetic, per_device(): contrib = jnp.sum(shares[:, :, None] * picked, axis=1)  6.02 us
  transfers between devices with their start and end apart: 5, of which 5 were waited for; matrix products, arithmetic and copies ran while one was open for 3% of the time, Pallas kernels for 0%

commit v1 on v0

--- a/solution.py
+++ b/solution.py
@@ -68,7 +68,9 @@
     ).astype(jnp.bfloat16)
     dispatch = jnp.dot(one_hot, normed, preferred_element_type=jnp.float32).astype(jnp.bfloat16)
     second = (row_ids >= lead_count).astype(jnp.bfloat16)
-    rows = lax.all_gather(dispatch, "fsdp", axis=0, tiled=True)
+    rows = jnp.concatenate(
+        lax.all_to_all(jnp.stack([dispatch] * lax.axis_size("fsdp")), "fsdp", 0, 0), axis=0
+    )
     labels = lax.all_gather(second, "fsdp", axis=0, tiled=True)
     gate = jnp.einsum("nd,edf->enf", rows, w_gate, preferred_element_type=jnp.float32)
     upper = jnp.einsum("nd,edf->enf", rows, w_up, preferred_element_type=jnp.float32)

time: 274 us -> 278 us (1.015)
  waiting for transfers between devices: 155 us -> 140 us
  blocking collectives: 40.8 us -> 55.5 us
  starting transfers between devices: 1.9 us -> 6.38 us
    all_gather x1 -> x0, waiting for transfers between devices: 17 us -> none  [per_device(): rows = lax.all_gather(dispatch, 'fsdp', axis=0, tiled=True)]
    unnamed x2, blocking collectives: 40.8 us -> 55.5 us
    all_to_all x0 -> x1, starting transfers between devices: none -> 4.6 us  [per_device(): lax.all_to_all(jnp.stack([dispatch] * lax.axis_size('fsdp')), 'fsdp', 0, 0)]
  transfers between devices with their start and end apart: 5 -> 5, of which waited for: 5 -> 5; matrix products, arithmetic and copies ran while one was open for 3% -> 2% of each run, Pallas kernels for 0% -> 0%
where the time goes in v1:
time: 278 us
  waiting for transfers between devices  140 us (50%)
  blocking collectives  55.5 us (20%)
  matrix products  40.6 us (15%)
  between operations  14.6 us (5%)
  other arithmetic  12.4 us (4%)
  local copies, waits for them, and re-layouts  7.97 us (3%)
  starting transfers between devices  6.38 us (2%)
    all_gather x1, waiting for transfers between devices, per_device(): lax.all_gather(out_weight, 'fsdp', axis=1, tiled=True)  81.3 us
    unnamed x2, blocking collectives  55.5 us
    psum x1, waiting for transfers between devices, per_device(): lax.psum(partial_attn.astype(jnp.bfloat16), 'expert').astype(jnp.float32)  31.4 us
    dot_general x1, matrix products, per_device(): jnp.einsum('enf,efd->nd', values_new, w_down, preferred_element_type=jnp....  22.2 us
    reduce_scatter x1, waiting for transfers between devices, per_device(): lax.psum_scatter(contrib.astype(jnp.bfloat16), 'expert', scatter_dimensio...  22.1 us
    dot_general x1, matrix products, per_device(): jnp.einsum('nd,edf->enf', rows, w_gate, preferred_element_type=jnp.float32)  12 us
    reduce_sum x1, other arithmetic, per_device(): contrib = jnp.sum(shares[:, :, None] * picked, axis=1)  6.02 us
  transfers between devices with their start and end apart: 5, of which 5 were waited for; matrix products, arithmetic and copies ran while one was open for 2% of the time, Pallas kernels for 0%

profile of v1, /device:TPU:0, one launch (start us, length us, event | category | flops | bytes accessed | tf_op | source)
XLA Modules:
  0.0 277.6 jit_solution(9931149364218960135)
XLA Ops:
  6.5 0.0 copy-start
  6.5 0.0 all-gather.2.cloned.1.call-start
  6.5 0.7 all-gather.2.cloned.1.call-update
  7.3 0.0 all-reduce.5.cloned.1.call-start
  7.3 0.1 iota_compare_fusion
  7.5 0.1 copy-done
  7.6 0.0 copy-start.8
  7.6 1.5 fusion.38
  9.1 0.5 fusion.12
  9.6 0.0 copy-done.8
  9.6 0.0 copy-start.4
  9.6 0.0 copy-start.7
  9.6 0.7 fusion.13
  10.3 0.1 copy.23
  10.4 0.0 copy-done.4
  10.4 0.6 fusion.34
  11.1 0.0 copy-done.7
  11.1 81.3 %all-gather.2.cloned.1.call-done = bf16[512,4096]{1,0:T(8,128)(2,1)} async-done(((bf16[512,1024]{1,0:T(8,128)(2,1)}), bf16[512,4096]{1,0:T(8,128)(2,1)}) %all-gather.2.cloned.1.call-update) | async-done | bytes 4194320 | tf_op jit(solution)/shard_map/all_gather | solution.py:51
  92.4 0.0 copy-start.5
  92.4 0.0 copy-start.3
  92.4 3.9 %convolution_convert_fusion = bf16[64,4096]{1,0:T(8,128)(2,1)} fusion(bf16[512,4096]{1,0:T(8,128)(2,1)} %all-gather.2.cloned.1.call-done, bf16[8,8,4,128]{3,2,1,0:T(4,128)(2,1)S(1)} %bitcast.72), kind=kOutput, calls=%fused_computation.3 | convolution fusion | flops 268697600 | bytes 4784128 | tf_op jit(solution)/shard_map/dot_general | solution.py:49
  96.3 0.0 copy-start.9
  96.3 0.0 all-reduce.5.cloned.1.call-update
  96.3 0.0 copy-done.5
  96.3 0.7 broadcast_select_fusion
  97.0 31.4 %all-reduce.5.cloned.1.call-done = bf16[64,4096]{1,0:T(8,128)(2,1)} async-done(((bf16[64,4096]{1,0:T(8,128)(2,1)}), bf16[64,4096]{1,0:T(8,128)(2,1)}) %all-reduce.5.cloned.1.call-update) | async-done | bytes 524304 | tf_op jit(solution)/shard_map/psum | solution.py:54
  128.4 0.0 copy-done.3
  128.4 1.3 fusion.14
  129.7 0.0 copy-start.2
  129.7 0.0 copy-done.9
  129.7 0.3 convolution_convert_fusion.1
  130.1 0.0 copy-start.6
  130.1 1.2 stack.16
  131.3 0.0 copy-done.2
  131.3 4.6 %all-to-all-start = ((bf16[4,36,4096]{2,1,0:T(8,128)(2,1)}), bf16[4,36,4096]{2,1,0:T(8,128)(2,1)S(1)}, u32[]{:S(2)}, u32[]{:S(2)}) async-start(bf16[4,36,4096]{2,1,0:T(8,128)(2,1)} %stack.16), calls=%async_computation | async-start | bytes 2621440 | tf_op jit(solution)/shard_map/all_to_all | solution.py:72
  135.9 0.0 reduce-scatter.4.cloned.1.call-start
  135.9 0.0 copy-done.6
  135.9 0.7 fusion.37
  137.1 0.7 compare_convert_fusion
  137.8 0.2 dynamic-update-slice
  138.0 24.3 %all-reduce = bf16[144]{0:T(256)(128)(2,1)S(1)} all-reduce(bf16[144]{0:T(256)(128)(2,1)S(1)} %dynamic-update-slice), channel_id=1, replica_groups=mesh['groups'=2,'fsdp'=4,'expert'=4] {'fsdp'}, use_global_device_ids=true, to_apply=%add | all-reduce | flops 144 | bytes 576
  162.4 0.7 compare_and_fusion
  163.0 0.1 copy.26
  163.1 0.1 reshape.69
  163.3 0.1 copy.25
  163.4 0.1 copy.24
  164.2 2.3 all-to-all-done
  166.5 1.1 reshape.84
  167.6 12.0 %convolution_bitcast_fusion.2 = f32[2,144,1792]{2,1,0:T(8,128)S(1)} fusion(bf16[144,4096,1]{1,0,2:T(8,128)(2,1)} %reshape.84, bf16[2,4096,1792]{2,1,0:T(8,128)(2,1)} %param.21), kind=kOutput, calls=%fused_computation.6 | convolution fusion | flops 4227858432 | bytes 32604160 | tf_op jit(solution)/shard_map/nd,edf->enf/dot_general | solution.py:75
  179.7 22.2 %fusion.1 = bf16[144,4096]{1,0:T(8,128)(2,1)} fusion(bf16[2,1792,4096]{2,1,0:T(8,128)(2,1)} %param.23, bf16[144,4096,1]{1,0,2:T(8,128)(2,1)} %reshape.84, bf16[2,4096,1792]{2,1,0:T(8,128)(2,1)} %param.22, f32[2,144,1792]{2,1,0:T(8,128)S(1)} %convolution_bitcast_fusion.2, f32[2,144]{1,0:T(2,128)S(1)} %pad_maximum_fusion), kind=kOutput, calls=%fused_computation.2 | convolution fusion | flops 8459919360 | bytes 63145088 | tf_op jit(solution)/shard_map/enf,efd->nd/dot_general | solution.py:81
  201.9 31.1 %fusion = bf16[40,4096]{1,0:T(8,128)(2,1)S(1)} fusion(bf16[144,4096]{1,0:T(8,128)(2,1)} %fusion.1), kind=kCustom, calls=%all-reduce-scatter | all-reduce-scatter fusion | flops 655361 | bytes 1507840
  233.0 1.7 collective-permute-start
  234.8 2.3 collective-permute-done
  237.1 0.4 concatenate
  237.5 0.1 dynamic-slice_convert_fusion
  237.6 1.3 gather_fusion
  238.9 0.0 copy-start.1
  239.0 2.3 reshape.68
  241.2 6.0 %multiply_reduce_fusion = bf16[64,4096]{1,0:T(8,128)(2,1)} fusion(f32[64,2,4096]{2,1,0:T(2,128)} %reshape.68, pred[64,2]{1,0:T(8,128)(4,1)S(1)} %copy.25, f32[64,2]{1,0:T(8,128)S(1)} %copy.24), kind=kLoop, calls=%fused_computation.13 | loop fusion | flops 1310720 | bytes 2622080 | tf_op jit(solution)/shard_map/reduce_sum | solution.py:92
  247.3 0.0 reduce-scatter.4.cloned.1.call-update
  247.3 22.1 %reduce-scatter.4.cloned.1.call-done = bf16[64,1024]{1,0:T(8,128)(2,1)} async-done(((bf16[64,4096]{1,0:T(8,128)(2,1)}), bf16[64,1024]{1,0:T(8,128)(2,1)}) %reduce-scatter.4.cloned.1.call-update) | async-done | bytes 131088 | tf_op jit(solution)/shard_map/reduce_scatter | solution.py:93
  269.4 1.7 add_convert_fusion.1
  271.1 0.0 copy-done.1
  (10 shorter events, 0.1 us)
Async XLA Ops:
  6.5 1.0 copy-start
  6.5 85.9 %all-gather.2.cloned.1.call-start = ((), (), s32[]{:S(2)}) async-start(), calls=%async_computation.2 | async-start | bytes 5242880 | tf_op jit(solution)/shard_map/all_gather | solution.py:51
  7.3 121.1 %all-reduce.5.cloned.1.call-start = ((), (), s32[]{:S(2)}) async-start(), calls=%async_computation.3 | async-start | bytes 1048576 | tf_op jit(solution)/shard_map/psum | solution.py:54
  7.6 2.0 copy-start.8
  9.6 0.8 copy-start.4
  9.6 1.5 copy-start.7
  92.4 3.9 %copy-start.5 = (s32[64,2]{0,1:T(2,128)S(1)}, s32[64,2]{0,1:T(2,128)}, u32[]{:S(2)}) copy-start(s32[64,2]{0,1:T(2,128)} %param.19) | copy-start | bytes 1540
  92.4 36.0 %copy-start.3 = (bf16[64,4096]{1,0:T(8,128)(2,1)S(1)}, bf16[64,4096]{1,0:T(8,128)(2,1)}, u32[]{:S(2)}) copy-start(bf16[64,4096]{1,0:T(8,128)(2,1)} %param.16) | copy-start | bytes 1572868
  96.3 33.4 %copy-start.9 = (f32[4096]{0:T(1024)S(1)}, f32[4096]{0:T(1024)}, u32[]{:S(2)}) copy-start(f32[4096]{0:T(1024)} %param.17) | copy-start | bytes 49156
  129.7 1.6 copy-start.2
  130.1 5.8 %copy-start.6 = (u32[32]{0:T(128)S(1)}, u32[32]{0:T(128)}, u32[]{:S(2)}) copy-start(u32[32]{0:T(128)} %constant.60) | copy-start | bytes 388
  131.3 35.2 %all-to-all-start = ((bf16[4,36,4096]{2,1,0:T(8,128)(2,1)}), bf16[4,36,4096]{2,1,0:T(8,128)(2,1)S(1)}, u32[]{:S(2)}, u32[]{:S(2)}) async-start(bf16[4,36,4096]{2,1,0:T(8,128)(2,1)} %stack.16), calls=%async_computation | async-start | bytes 2621440 | tf_op jit(solution)/shard_map/all_to_all | solution.py:72
  135.9 133.6 %reduce-scatter.4.cloned.1.call-start = ((), (), s32[]{:S(2)}) async-start(), calls=%async_computation.4 | async-start | bytes 655360 | tf_op jit(solution)/shard_map/reduce_scatter | solution.py:93
  233.0 4.1 %collective-permute-start = (bf16[12,4096]{1,0:T(8,128)(2,1)S(1)}, bf16[12,4096]{1,0:T(8,128)(2,1)S(1)}, u32[]{:S(2)}, u32[]{:S(2)}) collective-permute-start(bf16[12,4096]{1,0:T(8,128)(2,1)S(1)} %slice.10), channel_id=1, source_target_pairs={{0,4},{4,8},{8,12},{1,5},{5,9},{9,13},{2,6},{6,10},{10,14},{3,7},{... | collective-permute-start | bytes 294920
  238.9 32.2 %copy-start.1 = (bf16[1,2048,128]{2,1,0:T(8,128)(2,1)S(1)}, bf16[1,2048,128]{2,1,0:T(8,128)(2,1)}, u32[]{:S(2)}) copy-start(bf16[1,2048,128]{2,1,0:T(8,128)(2,1)} %param.13) | copy-start | bytes 1572868
Sparse Core Ops, SparseCore 0:
  8.9 83.4 all-gather.1
  96.4 31.8 all-reduce.4
  247.4 21.9 reduce-scatter.3
